TPU v7x, 32 devices: a whole 2x2x4 slice. The times are simulated.
32 devices in a mesh: gy: 16 (over z, x, core), gz: 2 (over y).
Axes of the slice: x: 2, y: 2, z: 4, core: 2. Of those that a mesh axis runs over, the one named last changes fastest.
Arguments:
- populations: float32 [19, 4, 128, 2048], P(None, None, 'gy', 'gz'), may hold values from 0 to 1, as said below
- solid_mask: int32 [4, 128, 2048], P(None, 'gy', 'gz'), may hold values 0 or 1
- body_force: float32 [3], replicated, may hold values from 0.002 to 0.008
Outputs:
- density: float32 [4, 128, 2048], P(None, 'gy', 'gz')
- velocity: float32 [3, 4, 128, 2048], P(None, None, 'gy', 'gz')
Inputs may be any that keep to these rules, and one draw needn't show every extreme that they name: `populations`: every population is positive, near its lattice weight times one.
All inputs are finite; a program needn't handle non-finite values. No bound on the sum of `solid_mask` on one device may be relied on, other than what follows from the above.
Results may differ from a plain program's by a relative error of at most 0.0003.
Values sent between devices are 32-bit elements; how exact they have to be, the bound alone decides.
A program may use at most 64 MiB of HBM per device.

v0:
```python
import functools

import jax
import jax.numpy as jnp
from jax import lax
from jax.experimental import pallas as pl
from jax.experimental.pallas import tpu as pltpu
from jax.sharding import PartitionSpec as P

STEPS = 3
W = 128

velocities = [
    (0, 0, 0),
    (1, 0, 0),
    (-1, 0, 0),
    (0, 1, 0),
    (0, -1, 0),
    (0, 0, 1),
    (0, 0, -1),
    (1, 1, 0),
    (-1, -1, 0),
    (1, -1, 0),
    (-1, 1, 0),
    (1, 0, 1),
    (-1, 0, -1),
    (1, 0, -1),
    (-1, 0, 1),
    (0, 1, 1),
    (0, -1, -1),
    (0, 1, -1),
    (0, -1, 1),
]
opposite = [0, 2, 1, 4, 3, 6, 5, 8, 7, 10, 9, 12, 11, 14, 13, 16, 15, 18, 17]
reference_mach = 0.05
Y_SET = {s: [k for k in range(19) if velocities[k][1] == s] for s in (1, -1)}
Z_SET = {s: [k for k in range(19) if velocities[k][2] == s] for s in (1, -1)}
ROUTES = [(1, 0), (-1, 0), (0, 1), (0, -1), (1, 1), (-1, 1), (1, -1), (-1, -1)]


def moments(f):
    s = [f[2 * a + 1] + f[2 * a + 2] for a in range(9)]
    d = [f[2 * a + 1] - f[2 * a + 2] for a in range(9)]
    axy, axz, ayz = s[3] + s[4], s[5] + s[6], s[7] + s[8]
    bxy, bxz, byz = s[3] - s[4], s[5] - s[6], s[7] - s[8]
    pxy, pxz, pyz = d[3] + d[4], d[5] + d[6], d[7] + d[8]
    qxy, qxz, qyz = d[3] - d[4], d[5] - d[6], d[7] - d[8]
    rho = (f[0] + s[0]) + (s[1] + s[2]) + ((axy + axz) + ayz)
    jx = d[0] + (pxy + pxz)
    jy = d[1] + (qxy + pyz)
    jz = d[2] + (qxz + qyz)
    return s, (axy, axz, ayz), (bxy, bxz, byz), (pxy, pxz, pyz), (qxy, qxz, qyz), rho, jx, jy, jz


def collide(f, force):
    s, (axy, axz, ayz), (bxy, bxz, byz), (pxy, pxz, pyz), (qxy, qxz, qyz), rho, jx, jy, jz = moments(f)
    inv = 1.0 / rho
    ux, uy, uz = jx * inv, jy * inv, jz * inv
    rxx, ryy, rzz = jx * ux, jy * uy, jz * uz
    third, ninth = rho * (1.0 / 3.0), rho * (1.0 / 9.0)
    e = 0.625
    exx = e * (s[0] + axy + axz - third - rxx)
    eyy = e * (s[1] + axy + ayz - third - ryy)
    ezz = e * (s[2] + axz + ayz - third - rzz)
    gxy = 0.5 * e * (bxy - jx * uy)
    gxz = 0.5 * e * (bxz - jx * uz)
    gyz = 0.5 * e * (byz - jy * uz)
    sq = (rxx + ryy + rzz) * (1.0 / 3.0)
    h = 0.65
    base = ninth + sq
    hxy = h * (axy - base + 0.5 * rzz)
    hxz = h * (axz - base + 0.5 * ryy)
    hyz = h * (ayz - base + 0.5 * rxx)
    t = 0.8
    jx3, jy3, jz3 = jx * (1.0 / 3.0), jy * (1.0 / 3.0), jz * (1.0 / 3.0)
    tpxy, tpxz, tpyz = t * (pxy - jx3), t * (pxz - jx3), t * (pyz - jy3)
    tqxy, tqxz, tqyz = t * (qxy - jy3), t * (qxz - jz3), t * (qyz - jz3)
    fx, fy, fz = force
    axis_w, edge_w = 3.0 / 18.0, 3.0 / 36.0
    even = [exx - hxy - hxz, eyy - hxy - hyz, ezz - hxz - hyz]
    odd = [-(tpxy + tpxz) - axis_w * fx, -(tqxy + tpyz) - axis_w * fy, -(tqxz + tqyz) - axis_w * fz]
    edges = (
        (hxy, gxy, tpxy, tqxy, fx, fy),
        (hxz, gxz, tpxz, tqxz, fx, fz),
        (hyz, gyz, tpyz, tqyz, fy, fz),
    )
    for hh, gg, tp, tq, fa, fb in edges:
        even += [0.5 * hh + gg, 0.5 * hh - gg]
        odd += [0.5 * (tp + tq) - edge_w * (fa + fb), 0.5 * (tp - tq) - edge_w * (fa - fb)]
    out = [f[0] + 2.0 * ((exx + eyy + ezz) - (hxy + hxz + hyz))]
    for a in range(9):
        out.append(f[2 * a + 1] - even[a] - odd[a])
        out.append(f[2 * a + 2] - even[a] + odd[a])
    return out


def kernel(gy, gz, pop_hbm, mask_hbm, force_ref, den_ref, vel_ref, raw, mask, bits, cells, ys, yh, zs, zh,
           mys, myh, mzs, mzh, load_sem, send_sem, recv_sem):
    planes, across, length = mask_hbm.shape
    chunks = length // W
    my, mz = lax.axis_index("gy"), lax.axis_index("gz")

    def peer(dy, dz):
        return {"gy": lax.rem(my + dy + gy, gy), "gz": lax.rem(mz + dz + gz, gz)}

    load_mask = pltpu.make_async_copy(mask_hbm, mask.at[:, :, W : W + length], load_sem.at[0])
    load_pop = pltpu.make_async_copy(pop_hbm, raw, load_sem.at[1])
    load_mask.start()
    load_pop.start()
    barrier = pltpu.get_barrier_semaphore()
    for dy, dz in ROUTES:
        pl.semaphore_signal(barrier, inc=1, device_id=peer(dy, dz), device_id_type=pl.DeviceIdType.MESH)

    lane = lax.broadcasted_iota(jnp.int32, (across, W), 1)
    sub = lax.broadcasted_iota(jnp.int32, (across, W), 0)
    edge_row = {1: across - 1, -1: 0}

    def copies(number, rows_out, rows_in, packed_out, packed_in):
        result = []
        for i, (dy, dz) in enumerate(ROUTES):
            if dz == 0:
                side = (1 - dy) // 2
                source, target = rows_out.at[side], rows_in.at[side, :, W : W + length]
            else:
                source, target = packed_out.at[(1 - dz) // 2], packed_in.at[i - 2]
            result.append(
                pltpu.make_async_remote_copy(
                    src_ref=source,
                    dst_ref=target,
                    send_sem=send_sem.at[number, i],
                    recv_sem=recv_sem.at[number, i],
                    device_id=peer(dy, dz),
                    device_id_type=pl.DeviceIdType.MESH,
                )
            )
        return result

    def pack_columns(items, first, zero):
        packed = zero
        for j, block in enumerate(items):
            shift = (j if first else j + 1) % W
            moved = pltpu.roll(block, shift, 1) if shift else block
            packed = jnp.where(lane == j, moved, packed)
        return packed

    def unpack(block, j, last):
        shift = (W - 1 - j if last else W - j) % W
        return pltpu.roll(block, shift, 1) if shift else block

    def pull(cell, row, c, base):
        cy, cz = c[1], c[2]

        def at(offset):
            v = cell(offset)
            if cy:
                v = jnp.where(sub == edge_row[cy], row(offset), v)
            return v

        v = at(base)
        if cz == 1:
            v = pltpu.roll(jnp.where(lane == W - 1, at(base - W), v), 1, 1)
        elif cz == -1:
            v = pltpu.roll(jnp.where(lane == 0, at(base + W), v), W - 1, 1)
        if cy:
            v = pltpu.roll(v, 1 if cy == 1 else across - 1, 0)
        return v

    load_mask.wait()
    for side, sign in enumerate((1, -1)):
        for p in range(planes):
            r = edge_row[sign]
            mys[side, p : p + 1, :] = mask[p, r : r + 1, W : W + length]
        offset = length if sign == 1 else W
        mzs[side] = pack_columns(
            [mask[p, :, offset : offset + W] for p in range(planes)], sign == -1, jnp.zeros((across, W), jnp.int32)
        )
    pl.semaphore_wait(barrier, len(ROUTES))
    mask_copies = copies(0, mys, myh, mzs, mzh)
    for copy in mask_copies:
        copy.start()

    force = (force_ref[0], force_ref[1], force_ref[2])

    def relax_and_store(step, f, p, base, into):
        relaxed = collide(f, force)
        for k in range(19):
            cells[into, k, p, :, pl.ds(base, W)] = relaxed[k]
        start = pl.multiple_of(base - W, W)
        for side, sign in enumerate((1, -1)):
            r = edge_row[sign]
            for i, k in enumerate(Y_SET[sign]):
                j = i * planes + p
                ys[step, side, j : j + 1, pl.ds(start, W)] = relaxed[k][r : r + 1, :]

    def send(step, into):
        for side, sign in enumerate((1, -1)):
            offset = length if sign == 1 else W
            zs[step, side] = pack_columns(
                [cells[into, k, p, :, offset : offset + W] for k in Z_SET[sign] for p in range(planes)],
                sign == -1,
                jnp.zeros((across, W), jnp.float32),
            )
        out = copies(1 + step, ys.at[step], yh.at[step], zs.at[step], zh.at[step])
        for copy in out:
            copy.start()
        return out

    def arrive(step, into, out):
        for copy in out:
            copy.wait_recv()
        for zside, zsign in enumerate((1, -1)):
            offset = 0 if zsign == 1 else W + length
            block = zh[step, ROUTES.index((0, zsign)) - 2]
            for i, k in enumerate(Z_SET[zsign]):
                for p in range(planes):
                    cells[into, k, p, :, offset : offset + W] = unpack(block, i * planes + p, zsign == 1)
            for yside, ysign in enumerate((1, -1)):
                corner = zh[step, ROUTES.index((ysign, zsign)) - 2]
                r = edge_row[ysign]
                k = velocities.index((0, ysign, zsign))
                for p in range(planes):
                    moved = unpack(corner, Z_SET[zsign].index(k) * planes + p, zsign == 1)
                    j = Y_SET[ysign].index(k) * planes + p
                    yh[step, yside, j : j + 1, offset : offset + W] = moved[r : r + 1, :]

    def streamed(step, into, p, base):
        flags = bits[p, :, pl.ds(pl.multiple_of(base - W, W), W)]
        f = []
        for k in range(19):
            c = velocities[k]
            here = cells[into, opposite[k], p, :, pl.ds(base, W)]
            q = p - c[0]
            if k == 0:
                moved = here
            elif q < 0 or q >= planes:
                f.append(here)
                continue
            else:

                def cell(offset, k=k, q=q):
                    return cells[into, k, q, :, pl.ds(pl.multiple_of(offset, W), W)]

                def row(offset, k=k, q=q, c=c):
                    j = Y_SET[c[1]].index(k) * planes + q
                    return yh[step, (1 - c[1]) // 2, j : j + 1, pl.ds(pl.multiple_of(offset, W), W)]

                moved = pull(cell, row, c, base)
            f.append(moved if k == 0 else jnp.where((flags & (1 << k)) != 0, here, moved))
        return f

    load_pop.wait()

    def first(i, carry):
        base = pl.multiple_of((i + 1) * W, W)
        for p in range(planes):
            f = [raw[k, p, :, pl.ds(pl.multiple_of(base - W, W), W)] for k in range(19)]
            relax_and_store(0, f, p, base, 0)
        return carry

    lax.fori_loop(0, chunks, first, 0)
    flying = send(0, 0)

    for copy in mask_copies:
        copy.wait_recv()
    for zside, zsign in enumerate((1, -1)):
        offset = 0 if zsign == 1 else W + length
        block = mzh[ROUTES.index((0, zsign)) - 2]
        for p in range(planes):
            mask[p, :, offset : offset + W] = unpack(block, p, zsign == 1)
        for yside, ysign in enumerate((1, -1)):
            corner = mzh[ROUTES.index((ysign, zsign)) - 2]
            r = edge_row[ysign]
            for p in range(planes):
                moved = unpack(corner, p, zsign == 1)
                myh[yside, p : p + 1, offset : offset + W] = moved[r : r + 1, :]

    def flag(i, carry):
        base = pl.multiple_of((i + 1) * W, W)
        shifted = {}
        for q in range(planes):

            def cell(offset, q=q):
                return mask[q, :, pl.ds(pl.multiple_of(offset, W), W)]

            for cy in (0, 1, -1):

                def row(offset, q=q, cy=cy):
                    return myh[(1 - cy) // 2, q : q + 1, pl.ds(pl.multiple_of(offset, W), W)]

                for cz in (0, 1, -1):
                    shifted[q, cy, cz] = pull(cell, row, (0, cy, cz), base)
        for p in range(planes):
            word = jnp.zeros((across, W), jnp.int32)
            for k in range(1, 19):
                c = velocities[k]
                q = p - c[0]
                if 0 <= q < planes:
                    word = word | jnp.where(shifted[q, c[1], c[2]] > 0, 1 << k, 0)
            bits[p, :, pl.ds(pl.multiple_of(base - W, W), W)] = word
        return carry

    lax.fori_loop(0, chunks, flag, 0)

    all_copies = [mask_copies, flying]
    for step in range(STEPS - 1):
        source, into = step % 2, (step + 1) % 2
        arrive(step, source, flying)

        def middle(i, carry, step=step, source=source, into=into):
            base = pl.multiple_of((i + 1) * W, W)
            for p in range(planes):
                relax_and_store(step + 1, streamed(step, source, p, base), p, base, into)
            return carry

        lax.fori_loop(0, chunks, middle, 0)
        flying = send(step + 1, into)
        all_copies.append(flying)

    last = (STEPS - 1) % 2
    arrive(STEPS - 1, last, flying)

    def final(i, carry):
        base = pl.multiple_of((i + 1) * W, W)
        spot = pl.ds(pl.multiple_of(base - W, W), W)
        for p in range(planes):
            f = streamed(STEPS - 1, last, p, base)
            rho, jx, jy, jz = moments(f)[-4:]
            fluid = (1 - mask[p, :, pl.ds(base, W)]).astype(jnp.float32)
            den_ref[p, :, spot] = rho * fluid
            scale = fluid * (1.0 / reference_mach) / rho
            vel_ref[0, p, :, spot] = jx * scale
            vel_ref[1, p, :, spot] = jy * scale
            vel_ref[2, p, :, spot] = jz * scale
        return carry

    lax.fori_loop(0, chunks, final, 0)
    for group in all_copies:
        for copy in group:
            copy.wait_send()


def solution(mesh):
    gy, gz = mesh.shape["gy"], mesh.shape["gz"]

    def local(populations, solid_mask, body_force):
        planes, across, length = solid_mask.shape
        rows = len(Y_SET[1]) * planes
        wide = length + 2 * W
        return pl.pallas_call(
            functools.partial(kernel, gy, gz),
            out_shape=(
                jax.ShapeDtypeStruct((planes, across, length), jnp.float32),
                jax.ShapeDtypeStruct((3, planes, across, length), jnp.float32),
            ),
            in_specs=[
                pl.BlockSpec(memory_space=pl.ANY),
                pl.BlockSpec(memory_space=pl.ANY),
                pl.BlockSpec(memory_space=pltpu.SMEM),
            ],
            out_specs=(pl.BlockSpec(memory_space=pltpu.VMEM), pl.BlockSpec(memory_space=pltpu.VMEM)),
            scratch_shapes=[
                pltpu.VMEM((19, planes, across, length), jnp.float32),
                pltpu.VMEM((planes, across, wide), jnp.int32),
                pltpu.VMEM((planes, across, length), jnp.int32),
                pltpu.VMEM((2, 19, planes, across, wide), jnp.float32),
                pltpu.VMEM((STEPS, 2, rows, length), jnp.float32),
                pltpu.VMEM((STEPS, 2, rows, wide), jnp.float32),
                pltpu.VMEM((STEPS, 2, across, W), jnp.float32),
                pltpu.VMEM((STEPS, 6, across, W), jnp.float32),
                pltpu.VMEM((2, planes, length), jnp.int32),
                pltpu.VMEM((2, planes, wide), jnp.int32),
                pltpu.VMEM((2, across, W), jnp.int32),
                pltpu.VMEM((6, across, W), jnp.int32),
                pltpu.SemaphoreType.DMA((2,)),
                pltpu.SemaphoreType.DMA((STEPS + 1, len(ROUTES))),
                pltpu.SemaphoreType.DMA((STEPS + 1, len(ROUTES))),
            ],
            compiler_params=pltpu.CompilerParams(collective_id=0, has_side_effects=True),
        )(populations, solid_mask, body_force)

    return jax.shard_map(
        local,
        mesh=mesh,
        in_specs=(P(None, None, "gy", "gz"), P(None, "gy", "gz"), P()),
        out_specs=(P(None, "gy", "gz"), P(None, None, "gy", "gz")),
        check_vma=False,
    )
```

profile of v0, /device:TPU:0, one launch (start us, length us, event | category | flops | bytes accessed | tf_op | source)
XLA Modules:
  0.0 36.9 jit_solution(6365402522015525267)
XLA Ops:
  0.6 33.0 %shard_map.50 = (f32[4,8,1024]{2,1,0:T(8,128)}, f32[3,4,8,1024]{3,2,1,0:T(8,128)}) custom-call(f32[19,4,8,1024]{3,2,1,0:T(8,128)} %pop_hbm.1, s32[4,8,1024]{2,1,0:T(8,128)} %mask_hbm.1, f32[3]{0:T(128)} %force_ref.1), custom_call_target="tpu_custom_call" | custom-call | tf_op jit(solution)/shard_map/pallas_call | solution.py:349
  33.6 1.6 %copy.7 = f32[4,8,1024]{2,1,0:T(8,128)} copy(f32[4,8,1024]{2,1,0:T(8,128)} %get-tuple-element.4) | data formatting | bytes 262144
  35.2 1.8 %copy.8 = f32[3,4,8,1024]{3,2,1,0:T(8,128)} copy(f32[3,4,8,1024]{3,2,1,0:T(8,128)} %get-tuple-element.5) | data formatting | bytes 786432
where the time goes:
time: 37.1 us; the launch traced here: 36.9 us
  Pallas kernels  33 us (89%)
  local copies, waits for them, and re-layouts  3.33 us (9%)
  between operations  0.64 us (2%)
    pallas_call x1, Pallas kernels, local(): pl.pallas_call(functools.partial(kernel, gy, gz), out_shape=(jax.ShapeDty...  33 us
    unnamed x2, local copies, waits for them, and re-layouts  3.33 us

commit v1 on v0

--- a/solution.py
+++ b/solution.py
@@ -9,6 +9,8 @@
 
 STEPS = 3
 W = 128
+UNROLL = 8
+VMEM_LIMIT = 24 << 20
 
 velocities = [
     (0, 0, 0),
@@ -94,7 +96,7 @@
     return out
 
 
-def kernel(gy, gz, pop_hbm, mask_hbm, force_ref, den_ref, vel_ref, raw, mask, bits, cells, ys, yh, zs, zh,
+def kernel(gy, gz, pop_hbm, mask_hbm, force_ref, out_ref, raw, mask, bits, cells, ys, yh, zs, zh,
            mys, myh, mzs, mzh, load_sem, send_sem, recv_sem):
     planes, across, length = mask_hbm.shape
     chunks = length // W
@@ -104,9 +106,10 @@
         return {"gy": lax.rem(my + dy + gy, gy), "gz": lax.rem(mz + dz + gz, gz)}
 
     load_mask = pltpu.make_async_copy(mask_hbm, mask.at[:, :, W : W + length], load_sem.at[0])
-    load_pop = pltpu.make_async_copy(pop_hbm, raw, load_sem.at[1])
+    load_pop = [pltpu.make_async_copy(pop_hbm.at[:, p], raw.at[p], load_sem.at[1 + p]) for p in range(planes)]
     load_mask.start()
-    load_pop.start()
+    for copy in load_pop:
+        copy.start()
     barrier = pltpu.get_barrier_semaphore()
     for dy, dz in ROUTES:
         pl.semaphore_signal(barrier, inc=1, device_id=peer(dy, dz), device_id_type=pl.DeviceIdType.MESH)
@@ -189,39 +192,36 @@
         for side, sign in enumerate((1, -1)):
             r = edge_row[sign]
             for i, k in enumerate(Y_SET[sign]):
-                j = i * planes + p
-                ys[step, side, j : j + 1, pl.ds(start, W)] = relaxed[k][r : r + 1, :]
-
-    def send(step, into):
+                ys[step, p, side, i : i + 1, pl.ds(start, W)] = relaxed[k][r : r + 1, :]
+
+    def send(step, into, p):
         for side, sign in enumerate((1, -1)):
             offset = length if sign == 1 else W
-            zs[step, side] = pack_columns(
-                [cells[into, k, p, :, offset : offset + W] for k in Z_SET[sign] for p in range(planes)],
+            zs[step, p, side] = pack_columns(
+                [cells[into, k, p, :, offset : offset + W] for k in Z_SET[sign]],
                 sign == -1,
                 jnp.zeros((across, W), jnp.float32),
             )
-        out = copies(1 + step, ys.at[step], yh.at[step], zs.at[step], zh.at[step])
+        out = copies(1 + step * planes + p, ys.at[step, p], yh.at[step, p], zs.at[step, p], zh.at[step, p])
         for copy in out:
             copy.start()
         return out
 
-    def arrive(step, into, out):
+    def arrive(step, into, out, p):
         for copy in out:
             copy.wait_recv()
-        for zside, zsign in enumerate((1, -1)):
+        for zsign in (1, -1):
             offset = 0 if zsign == 1 else W + length
-            block = zh[step, ROUTES.index((0, zsign)) - 2]
+            block = zh[step, p, ROUTES.index((0, zsign)) - 2]
             for i, k in enumerate(Z_SET[zsign]):
-                for p in range(planes):
-                    cells[into, k, p, :, offset : offset + W] = unpack(block, i * planes + p, zsign == 1)
+                cells[into, k, p, :, offset : offset + W] = unpack(block, i, zsign == 1)
             for yside, ysign in enumerate((1, -1)):
-                corner = zh[step, ROUTES.index((ysign, zsign)) - 2]
+                corner = zh[step, p, ROUTES.index((ysign, zsign)) - 2]
                 r = edge_row[ysign]
                 k = velocities.index((0, ysign, zsign))
-                for p in range(planes):
-                    moved = unpack(corner, Z_SET[zsign].index(k) * planes + p, zsign == 1)
-                    j = Y_SET[ysign].index(k) * planes + p
-                    yh[step, yside, j : j + 1, offset : offset + W] = moved[r : r + 1, :]
+                moved = unpack(corner, Z_SET[zsign].index(k), zsign == 1)
+                j = Y_SET[ysign].index(k)
+                yh[step, p, yside, j : j + 1, offset : offset + W] = moved[r : r + 1, :]
 
     def streamed(step, into, p, base):
         flags = bits[p, :, pl.ds(pl.multiple_of(base - W, W), W)]
@@ -241,24 +241,33 @@
                     return cells[into, k, q, :, pl.ds(pl.multiple_of(offset, W), W)]
 
                 def row(offset, k=k, q=q, c=c):
-                    j = Y_SET[c[1]].index(k) * planes + q
-                    return yh[step, (1 - c[1]) // 2, j : j + 1, pl.ds(pl.multiple_of(offset, W), W)]
+                    j = Y_SET[c[1]].index(k)
+                    return yh[step, q, (1 - c[1]) // 2, j : j + 1, pl.ds(pl.multiple_of(offset, W), W)]
 
                 moved = pull(cell, row, c, base)
             f.append(moved if k == 0 else jnp.where((flags & (1 << k)) != 0, here, moved))
         return f
 
-    load_pop.wait()
-
-    def first(i, carry):
-        base = pl.multiple_of((i + 1) * W, W)
-        for p in range(planes):
-            f = [raw[k, p, :, pl.ds(pl.multiple_of(base - W, W), W)] for k in range(19)]
+    unroll = max(u for u in (UNROLL, 4, 2, 1) if chunks % u == 0)
+
+    def over_chunks(block):
+        def group(i, carry):
+            for n in range(unroll):
+                block(pl.multiple_of((i * unroll + (n + 1)) * W, W))
+            return carry
+
+        lax.fori_loop(0, chunks // unroll, group, 0)
+
+    flying = []
+    for p in range(planes):
+        load_pop[p].wait()
+
+        def first(base, p=p):
+            f = [raw[p, k, :, pl.ds(pl.multiple_of(base - W, W), W)] for k in range(19)]
             relax_and_store(0, f, p, base, 0)
-        return carry
-
-    lax.fori_loop(0, chunks, first, 0)
-    flying = send(0, 0)
+
+        over_chunks(first)
+        flying.append(send(0, 0, p))
 
     for copy in mask_copies:
         copy.wait_recv()
@@ -301,82 +310,96 @@
 
     lax.fori_loop(0, chunks, flag, 0)
 
-    all_copies = [mask_copies, flying]
-    for step in range(STEPS - 1):
+    all_copies = [mask_copies] + flying
+    for step in range(STEPS):
         source, into = step % 2, (step + 1) % 2
-        arrive(step, source, flying)
-
-        def middle(i, carry, step=step, source=source, into=into):
-            base = pl.multiple_of((i + 1) * W, W)
-            for p in range(planes):
+        started = []
+        arrived = 0
+        for p in range(planes):
+            while arrived < min(p + 2, planes):
+                arrive(step, source, flying[arrived], arrived)
+                arrived += 1
+
+            def middle(base, p=p, step=step, source=source, into=into):
                 relax_and_store(step + 1, streamed(step, source, p, base), p, base, into)
-            return carry
-
-        lax.fori_loop(0, chunks, middle, 0)
-        flying = send(step + 1, into)
-        all_copies.append(flying)
-
-    last = (STEPS - 1) % 2
-    arrive(STEPS - 1, last, flying)
-
-    def final(i, carry):
-        base = pl.multiple_of((i + 1) * W, W)
-        spot = pl.ds(pl.multiple_of(base - W, W), W)
-        for p in range(planes):
-            f = streamed(STEPS - 1, last, p, base)
-            rho, jx, jy, jz = moments(f)[-4:]
-            fluid = (1 - mask[p, :, pl.ds(base, W)]).astype(jnp.float32)
-            den_ref[p, :, spot] = rho * fluid
-            scale = fluid * (1.0 / reference_mach) / rho
-            vel_ref[0, p, :, spot] = jx * scale
-            vel_ref[1, p, :, spot] = jy * scale
-            vel_ref[2, p, :, spot] = jz * scale
-        return carry
-
-    lax.fori_loop(0, chunks, final, 0)
+
+            def final(base, p=p, step=step, source=source):
+                spot = pl.ds(pl.multiple_of(base - W, W), W)
+                rho, jx, jy, jz = moments(streamed(step, source, p, base))[-4:]
+                fluid = (1 - mask[p, :, pl.ds(base, W)]).astype(jnp.float32)
+                scale = fluid * (1.0 / reference_mach) / rho
+                out_ref[0, p, :, spot] = rho * fluid
+                out_ref[1, p, :, spot] = jx * scale
+                out_ref[2, p, :, spot] = jy * scale
+                out_ref[3, p, :, spot] = jz * scale
+
+            if step < STEPS - 1:
+                over_chunks(middle)
+                started.append(send(step + 1, into, p))
+            else:
+                over_chunks(final)
+        flying = started
+        all_copies += flying
     for group in all_copies:
         for copy in group:
             copy.wait_send()
 
 
+def hand_out(both_ref, den_hbm, vel_hbm, sem):
+    den = pltpu.make_async_copy(both_ref.at[0], den_hbm, sem.at[0])
+    vel = pltpu.make_async_copy(both_ref.at[pl.ds(1, 3)], vel_hbm, sem.at[1])
+    vel.start()
+    den.start()
+    vel.wait()
+    den.wait()
+
+
 def solution(mesh):
     gy, gz = mesh.shape["gy"], mesh.shape["gz"]
 
     def local(populations, solid_mask, body_force):
         planes, across, length = solid_mask.shape
-        rows = len(Y_SET[1]) * planes
+        rows = len(Y_SET[1])
         wide = length + 2 * W
+        both = pl.pallas_call(
+            functools.partial(kernel, gy, gz),
+            out_shape=jax.ShapeDtypeStruct((4, planes, across, length), jnp.float32),
+            in_specs=[
+                pl.BlockSpec(memory_space=pltpu.HBM),
+                pl.BlockSpec(memory_space=pltpu.HBM),
+                pl.BlockSpec(memory_space=pltpu.SMEM),
+            ],
+            out_specs=pl.BlockSpec(memory_space=pltpu.VMEM),
+            scratch_shapes=[
+                pltpu.VMEM((planes, 19, across, length), jnp.float32),
+                pltpu.VMEM((planes, across, wide), jnp.int32),
+                pltpu.VMEM((planes, across, length), jnp.int32),
+                pltpu.VMEM((2, 19, planes, across, wide), jnp.float32),
+                pltpu.VMEM((STEPS, planes, 2, rows, length), jnp.float32),
+                pltpu.VMEM((STEPS, planes, 2, rows, wide), jnp.float32),
+                pltpu.VMEM((STEPS, planes, 2, across, W), jnp.float32),
+                pltpu.VMEM((STEPS, planes, 6, across, W), jnp.float32),
+                pltpu.VMEM((2, planes, length), jnp.int32),
+                pltpu.VMEM((2, planes, wide), jnp.int32),
+                pltpu.VMEM((2, across, W), jnp.int32),
+                pltpu.VMEM((6, across, W), jnp.int32),
+                pltpu.SemaphoreType.DMA((1 + planes,)),
+                pltpu.SemaphoreType.DMA((STEPS * planes + 1, len(ROUTES))),
+                pltpu.SemaphoreType.DMA((STEPS * planes + 1, len(ROUTES))),
+            ],
+            compiler_params=pltpu.CompilerParams(collective_id=0, has_side_effects=True, vmem_limit_bytes=VMEM_LIMIT),
+        )(populations, solid_mask, body_force)
         return pl.pallas_call(
-            functools.partial(kernel, gy, gz),
+            hand_out,
             out_shape=(
                 jax.ShapeDtypeStruct((planes, across, length), jnp.float32),
                 jax.ShapeDtypeStruct((3, planes, across, length), jnp.float32),
             ),
-            in_specs=[
-                pl.BlockSpec(memory_space=pl.ANY),
-                pl.BlockSpec(memory_space=pl.ANY),
-                pl.BlockSpec(memory_space=pltpu.SMEM),
-            ],
-            out_specs=(pl.BlockSpec(memory_space=pltpu.VMEM), pl.BlockSpec(memory_space=pltpu.VMEM)),
-            scratch_shapes=[
-                pltpu.VMEM((19, planes, across, length), jnp.float32),
-                pltpu.VMEM((planes, across, wide), jnp.int32),
-                pltpu.VMEM((planes, across, length), jnp.int32),
-                pltpu.VMEM((2, 19, planes, across, wide), jnp.float32),
-                pltpu.VMEM((STEPS, 2, rows, length), jnp.float32),
-                pltpu.VMEM((STEPS, 2, rows, wide), jnp.float32),
-                pltpu.VMEM((STEPS, 2, across, W), jnp.float32),
-                pltpu.VMEM((STEPS, 6, across, W), jnp.float32),
-                pltpu.VMEM((2, planes, length), jnp.int32),
-                pltpu.VMEM((2, planes, wide), jnp.int32),
-                pltpu.VMEM((2, across, W), jnp.int32),
-                pltpu.VMEM((6, across, W), jnp.int32),
-                pltpu.SemaphoreType.DMA((2,)),
-                pltpu.SemaphoreType.DMA((STEPS + 1, len(ROUTES))),
-                pltpu.SemaphoreType.DMA((STEPS + 1, len(ROUTES))),
-            ],
-            compiler_params=pltpu.CompilerParams(collective_id=0, has_side_effects=True),
-        )(populations, solid_mask, body_force)
+            in_specs=[pl.BlockSpec(memory_space=pltpu.VMEM)],
+            out_specs=(pl.BlockSpec(memory_space=pl.ANY), pl.BlockSpec(memory_space=pl.ANY)),
+            scratch_shapes=[pltpu.SemaphoreType.DMA((2,))],
+            compiler_params=pltpu.CompilerParams(vmem_limit_bytes=VMEM_LIMIT),
+        )(both)
 
     return jax.shard_map(
         local,

time: 37.1 us -> 29.3 us (0.79)
  Pallas kernels: 33 us -> 25.2 us
    pallas_call x1 -> x2, Pallas kernels: 33 us -> 25.2 us  [the longest x1 24.4 us: local(): pl.pallas_call(functools.partial(kernel, gy, gz), out_shape=jax.ShapeDtyp...]
    unnamed x2 -> x6, local copies, waits for them, and re-layouts: 3.33 us -> 3.25 us
where the time goes in v1:
time: 29.3 us; the launch traced here: 29.1 us
  Pallas kernels  25.2 us (86%)
  local copies, waits for them, and re-layouts  3.25 us (11%)
  between operations  0.65 us (2%)
    pallas_call x1, Pallas kernels, local(): pl.pallas_call(functools.partial(kernel, gy, gz), out_shape=jax.ShapeDtyp...  24.4 us
    unnamed x6, local copies, waits for them, and re-layouts  3.25 us
    pallas_call x1, Pallas kernels, local(): pl.pallas_call(hand_out, out_shape=(jax.ShapeDtypeStruct((planes, across,...  0.8 us

profile of v1, /device:TPU:0, one launch (start us, length us, event | category | flops | bytes accessed | tf_op | source)
XLA Modules:
  0.0 29.1 jit_solution(12844452559688870988)
XLA Ops:
  0.6 0.0 copy-start
  0.6 1.7 %copy-done = f32[19,4,8,1024]{3,2,1,0:T(8,128)S(1)} copy-done((f32[19,4,8,1024]{3,2,1,0:T(8,128)S(1)}, f32[19,4,8,1024]{3,2,1,0:T(8,128)}, u32[]{:S(2)}) %copy-start) | copy-done | bytes 2490392
  2.3 0.0 copy-start.1
  2.3 0.9 %copy-done.1 = s32[4,8,1024]{2,1,0:T(8,128)S(1)} copy-done((s32[4,8,1024]{2,1,0:T(8,128)S(1)}, s32[4,8,1024]{2,1,0:T(8,128)}, u32[]{:S(2)}) %copy-start.1) | copy-done | bytes 131096
  3.2 0.0 copy-start.2
  3.2 0.7 %copy-done.2 = f32[3]{0:T(128)S(1)} copy-done((f32[3]{0:T(128)S(1)}, f32[3]{0:T(128)}, u32[]{:S(2)}) %copy-start.2) | copy-done | bytes 36
  3.9 24.4 %shard_map.50.both_ref = f32[4,4,8,1024]{3,2,1,0:T(8,128)S(1)} custom-call(f32[19,4,8,1024]{3,2,1,0:T(8,128)S(1)} %copy-done, s32[4,8,1024]{2,1,0:T(8,128)S(1)} %copy-done.1, f32[3]{0:T(128)S(1)} %copy-done.2), custom_call_target="tpu_custom_call" | custom-call | tf_op jit(solution)/shard_map/pallas_call | solution.py:364
  28.3 0.8 %shard_map.51 = (f32[4,8,1024]{2,1,0:T(8,128)}, f32[3,4,8,1024]{3,2,1,0:T(8,128)}) custom-call(f32[4,4,8,1024]{3,2,1,0:T(8,128)S(1)} %shard_map.50.both_ref), custom_call_target="tpu_custom_call" | custom-call | tf_op jit(solution)/shard_map/pallas_call | solution.py:392
Async XLA Ops:
  0.6 1.7 %copy-start = (f32[19,4,8,1024]{3,2,1,0:T(8,128)S(1)}, f32[19,4,8,1024]{3,2,1,0:T(8,128)}, u32[]{:S(2)}) copy-start(f32[19,4,8,1024]{3,2,1,0:T(8,128)} %pop_hbm.1) | copy-start | bytes 7471108
  2.3 0.9 %copy-start.1 = (s32[4,8,1024]{2,1,0:T(8,128)S(1)}, s32[4,8,1024]{2,1,0:T(8,128)}, u32[]{:S(2)}) copy-start(s32[4,8,1024]{2,1,0:T(8,128)} %mask_hbm.1) | copy-start | bytes 393220
  3.2 0.7 %copy-start.2 = (f32[3]{0:T(128)S(1)}, f32[3]{0:T(128)}, u32[]{:S(2)}) copy-start(f32[3]{0:T(128)} %force_ref.1) | copy-start | bytes 40
